TPU v7x, 32 devices: a whole 2x2x4 slice. The times are simulated.
32 devices in a mesh: samples: 8 (over z, y), variants: 4 (over x, core).
Axes of the slice: x: 2, y: 2, z: 4, core: 2. Of those that a mesh axis runs over, the one named last changes fastest.
Arguments:
- genotypes: int32 [2048, 32768], P('variants', 'samples'), may hold values from 0 to 3, as said below
- weights: float32 [32768], P('samples'), may hold values from 0.25 to 20
Outputs:
- call_mean: float32 [2048], P('variants')
- call_var: float32 [2048], P('variants')
- class_counts: int32 [4, 2048], P(None, 'variants')
- ld_window: float32 [1024, 2048], P('samples', 'variants')
- sample_calls: int32 [2, 32768], P(None, 'samples')
- sample_share: float32 [32768], P('samples')
Inputs may be any that keep to these rules, and one draw needn't show every extreme that they name: `genotypes`: in every variant's row, each aligned group of 8 samples (samples 8 i to 8 i + 7) holds at least one call other than 3.
All inputs are finite; a program needn't handle non-finite values.
Results may differ from a plain program's by a relative error of at most 0.0004.
Values may be sent and summed in bfloat16 or wider, within the bound.
A program may use at most 64 MiB of HBM per device.

v0:
```python
import jax
import jax.numpy as jnp
from jax import lax
from jax.sharding import PartitionSpec as P


def shifted(value, axis, by):
    size = lax.axis_size(axis)
    pairs = [(i, i + by) for i in range(size) if 0 <= i + by < size]
    return lax.ppermute(value, axis, pairs)


def on_device(genotypes, weights):
    present = genotypes != 3
    called = present.astype(jnp.float32)
    dosage = jnp.where(present, genotypes, 0).astype(jnp.float32)
    weighted = called * weights[None, :]
    w_sum_part = jnp.sum(weighted, axis=1)
    first_part = jnp.sum(weighted * dosage, axis=1)
    classes = jnp.stack(
        [jnp.sum((genotypes == level).astype(jnp.float32), axis=1) for level in range(4)]
    )
    second_part = jnp.sum(weighted * dosage * dosage, axis=1)
    w_sum, first_total, second_total, class_total = lax.psum(
        (w_sum_part, first_part, second_part, classes), "samples"
    )
    mean_value = first_total / w_sum
    deviation = second_total - first_total * mean_value
    var_value = deviation / w_sum
    factor = 1.0 / jnp.sqrt(w_sum * (var_value + 1e-05))
    centered = (dosage - mean_value[:, None]) * called
    scaled = (jnp.sqrt(weights)[None, :] * centered * factor[:, None]).astype(jnp.bfloat16)
    following = shifted(scaled, "variants", -1)
    joined = jnp.concatenate([scaled, following], axis=0)
    rows_owned = joined.shape[0] // lax.axis_size("samples")
    partial_all = lax.dot_general(
        joined, scaled, (((1,), (1,)), ((), ())), preferred_element_type=jnp.float32
    )
    summed = lax.psum(partial_all, "samples")
    ld_window = lax.dynamic_slice_in_dim(
        summed, lax.axis_index("samples") * rows_owned, rows_owned, 0
    )
    squares = scaled.astype(jnp.float32)
    called_total, het_total, square_total = lax.psum(
        (
            jnp.sum(called, axis=0),
            jnp.sum((genotypes == 1).astype(jnp.float32), axis=0),
            jnp.sum(squares * squares, axis=0),
        ),
        "variants",
    )
    samples_all = weights.shape[0] * lax.axis_size("samples")
    variants_all = genotypes.shape[0] * lax.axis_size("variants")
    sample_share = square_total * (samples_all / variants_all)
    sample_calls = jnp.stack([called_total, het_total]).astype(jnp.int32)
    return (
        mean_value,
        var_value,
        class_total.astype(jnp.int32),
        ld_window,
        sample_calls,
        sample_share,
    )


def solution(mesh):
    placed = (P("variants", "samples"), P("samples"))
    return jax.shard_map(
        on_device,
        mesh=mesh,
        in_specs=placed,
        out_specs=(
            P("variants"),
            P("variants"),
            P(None, "variants"),
            P("samples", "variants"),
            P(None, "samples"),
            P("samples"),
        ),
        check_vma=False,
    )
```

profile of v0, /device:TPU:0, one launch (start us, length us, event | category | flops | bytes accessed | tf_op | source)
XLA Modules:
  0.0 226.3 jit_solution(9397429142286188237)
XLA Ops:
  7.2 0.0 copy-start.1
  7.2 0.0 all-reduce.4.cloned.1.call-start
  7.2 0.0 copy-start
  7.2 5.0 %convert_reduce_fusion = (f32[4096]{0:T(1024)S(1)}, f32[512]{0:T(512)S(1)}) fusion(s32[512,4096]{1,0:T(8,128)} %param.2), kind=kLoop, calls=%fused_computation | loop fusion | flops 8384000 | bytes 8407040 | tf_op jit(solution)/shard_map/reduce_sum | solution.py:47
  12.3 0.0 copy-done.1
  12.3 0.7 copy-done
  13.0 6.3 %fusion.2 = (f32[512]{0:T(512)S(1)}, f32[512]{0:T(512)S(1)}, f32[512]{0:T(512)S(1)}, f32[4096]{0:T(1024)S(1)}, f32[512]{0:T(512)S(1)}, /*index=5*/f32[512]{0:T(512)S(1)}, f32[512]{0:T(512)S(1)}) fusion(s32[512,4096]{1,0:T(8,128)S(1)} %copy-done, f32[4096]{0:T(1024)S(1)} %copy-done.1), kind=kLoop, calls=%fused_computation.6 | loop fusion | flops 41935872 | bytes 8433664 | tf_op jit(solution)/shard_map/reduce_sum | solution.py:23
  19.4 38.9 %all-reduce = (f32[512]{0:T(512)S(1)}, f32[512]{0:T(512)S(1)}, f32[512]{0:T(512)S(1)}, f32[4,512]{1,0:T(4,128)S(1)}) all-reduce(f32[512]{0:T(512)S(1)} %get-tuple-element.8, f32[512]{0:T(512)S(1)} %get-tuple-element.7, f32[512]{0:T(512)S(1)} %get-tuple-element.6, ...), channel_id=1, replica_groups=mesh['samples'=8,'variants'=4] {'samples'}, use_global_device_ids=true, to_apply=%region_1.2 | all-reduce | flops 3584 | bytes 28672 | tf_op jit(solution)/shard_map/psum | solution.py:24
  58.2 0.6 multiply_rsqrt_fusion
  58.8 0.0 copy-start.2
  58.8 5.2 %multiply_reduce_fusion = (f32[4096]{0:T(1024)S(1)}, bf16[512,4096]{1,0:T(8,128)(2,1)S(1)}) fusion(f32[512]{0:T(512)S(1)} %get-tuple-element.24, f32[512]{0:T(512)S(1)} %get-tuple-element.26, s32[512,4096]{1,0:T(8,128)} %param.2, f32[4096]{0:T(1024)S(1)} %sqrt.6), kind=kLoop, calls=%fused_computation.11 | loop fusion | flops 23064576 | bytes 12619776 | tf_op jit(solution)/shard_map/reduce_sum | solution.py:48
  64.0 1.3 collective-permute-start
  65.3 7.8 %collective-permute-done = bf16[512,4096]{1,0:T(8,128)(2,1)S(1)} collective-permute-done((bf16[512,4096]{1,0:T(8,128)(2,1)S(1)}, bf16[512,4096]{1,0:T(8,128)(2,1)S(1)}, u32[]{:S(2)}, u32[]{:S(2)}) %collective-permute-start) | collective-permute-done | bytes 4194336 | tf_op jit(solution)/shard_map/ppermute | solution.py:10
  73.1 5.8 %fusion.3 = f32[1024,512]{1,0:T(8,128)} fusion(bf16[512,4096]{1,0:T(8,128)(2,1)S(1)} %get-tuple-element.23, bf16[512,4096]{1,0:T(8,128)(2,1)S(1)} %collective-permute-done), kind=kOutput, calls=%fused_computation.7 | convolution fusion | flops 4311744512 | bytes 10485760 | tf_op jit(solution)/shard_map/dot_general | solution.py:36
  78.9 0.0 copy-done.2
  78.9 0.0 all-reduce.4.cloned.1.call-update
  78.9 0.6 convert_element_type.36
  79.5 51.9 %all-reduce.1 = (f32[1,4096]{1,0:T(1,128)S(1)}, f32[1,4096]{1,0:T(1,128)S(1)}, f32[4096]{0:T(1024)S(1)}) all-reduce(f32[1,4096]{1,0:T(1,128)S(1)} %bitcast.7, f32[1,4096]{1,0:T(1,128)S(1)} %bitcast.8, f32[4096]{0:T(1024)S(1)} %get-tuple-element.22), channel_id=1, replica_groups=mesh['samples'=8,'variants'=4] {'variants'}, use_global_device_ids=true, to_apply=%region_15.16 | all-reduce | flops 12288 | bytes 98304 | tf_op jit(solution)/shard_map/psum | solution.py:44
  131.4 0.6 broadcast_multiply_fusion
  132.0 0.7 maximum_convert_fusion
  132.7 85.1 %all-reduce.4.cloned.1.call-done = f32[1024,512]{1,0:T(8,128)} async-done(((f32[1024,512]{1,0:T(8,128)}), f32[1024,512]{1,0:T(8,128)}) %all-reduce.4.cloned.1.call-update) | async-done | bytes 2097168 | tf_op jit(solution)/shard_map/psum | solution.py:39
  217.8 1.7 constant_dynamic-slice_fusion
  (2 shorter events, 0.0 us)
Async XLA Ops:
  7.2 5.1 %copy-start.1 = (f32[4096]{0:T(1024)S(1)}, f32[4096]{0:T(1024)}, u32[]{:S(2)}) copy-start(f32[4096]{0:T(1024)} %param.3) | copy-start | bytes 49156
  7.2 210.6 %all-reduce.4.cloned.1.call-start = ((), (), s32[]{:S(2)}) async-start(), calls=%async_computation | async-start | bytes 4194304 | tf_op jit(solution)/shard_map/psum | solution.py:39
  7.2 5.8 %copy-start = (s32[512,4096]{1,0:T(8,128)S(1)}, s32[512,4096]{1,0:T(8,128)}, u32[]{:S(2)}) copy-start(s32[512,4096]{1,0:T(8,128)} %param.2) | copy-start | bytes 25165828
  58.8 20.0 %copy-start.2 = (f32[512]{0:T(512)}, f32[512]{0:T(512)S(1)}, u32[]{:S(2)}) copy-start(f32[512]{0:T(512)S(1)} %get-tuple-element.26) | copy-start | bytes 6148
  64.0 9.1 %collective-permute-start = (bf16[512,4096]{1,0:T(8,128)(2,1)S(1)}, bf16[512,4096]{1,0:T(8,128)(2,1)S(1)}, u32[]{:S(2)}, u32[]{:S(2)}) collective-permute-start(bf16[512,4096]{1,0:T(8,128)(2,1)S(1)} %get-tuple-element.23), channel_id=1, source_target_pairs={{1,0},{2,1},{3,2},{5,4},{6,5},{7,6},{9,8},{10,9},{11,10},{13,12},{... | collective-permute-start | bytes 12582920 | tf_op jit(solution)/shard_map/ppermute | solution.py:10
Sparse Core Ops, SparseCore 0:
  79.0 138.7 all-reduce.3
where the time goes:
time: 227 us; the launch traced here: 226 us
  waiting for transfers between devices  92.8 us (41%)
  blocking collectives  90.8 us (40%)
  other arithmetic  19 us (8%)
  between operations  14.1 us (6%)
  matrix products  5.81 us (3%)
  local copies, waits for them, and re-layouts  2.4 us (1%)
    psum x1, waiting for transfers between devices, on_device(): summed = lax.psum(partial_all, 'samples')  85.1 us
    psum x1, blocking collectives, on_device(): lax.psum((jnp.sum(called, axis=0), jnp.sum((genotypes == 1).astype(jnp.fl...  51.9 us
    psum x1, blocking collectives, on_device(): lax.psum((w_sum_part, first_part, second_part, classes), 'samples')  38.9 us
    ppermute x1, waiting for transfers between devices, shifted(): return lax.ppermute(value, axis, pairs)  7.75 us
    reduce_sum x1, other arithmetic, on_device(): second_part = jnp.sum(weighted * dosage * dosage, axis=1)  6.32 us
    dot_general x1, matrix products, on_device(): lax.dot_general(joined, scaled, (((1,), (1,)), ((), ())), preferred_eleme...  5.81 us
    reduce_sum x1, other arithmetic, on_device(): jnp.sum(squares * squares, axis=0)  5.17 us
    reduce_sum x1, other arithmetic, on_device(): jnp.sum((genotypes == 1).astype(jnp.float32), axis=0)  5.04 us
  transfers between devices with their start and end apart: 2, of which 2 were waited for; matrix products, arithmetic and copies ran while one was open for 1% of the time, Pallas kernels for 0%

commit v1 on v0

--- a/solution.py
+++ b/solution.py
@@ -36,7 +36,8 @@
     partial_all = lax.dot_general(
         joined, scaled, (((1,), (1,)), ((), ())), preferred_element_type=jnp.float32
     )
-    summed = lax.psum(partial_all, "samples")
+    parts = lax.all_gather(partial_all, "samples", axis=0, tiled=False)
+    summed = parts.sum(axis=0)
     ld_window = lax.dynamic_slice_in_dim(
         summed, lax.axis_index("samples") * rows_owned, rows_owned, 0
     )

time: 227 us -> 359 us (1.58)
  waiting for transfers between devices: 92.8 us -> 218 us
  other arithmetic: 19 us -> 27.1 us
    all_gather x0 -> x1, waiting for transfers between devices: none -> 210 us  [on_device(): parts = lax.all_gather(partial_all, 'samples', axis=0, tiled=False)]
    psum x1 -> x0, waiting for transfers between devices: 85.1 us -> none  [on_device(): summed = lax.psum(partial_all, 'samples')]
    reduce_sum x0 -> x1, other arithmetic: none -> 8.08 us  [on_device(): summed = parts.sum(axis=0)]
where the time goes in v1:
time: 359 us; the launch traced here: 358 us
  waiting for transfers between devices  218 us (61%)
  blocking collectives  90.4 us (25%)
  other arithmetic  27.1 us (8%)
  between operations  14.1 us (4%)
  matrix products  5.87 us (2%)
    all_gather x1, waiting for transfers between devices, on_device(): parts = lax.all_gather(partial_all, 'samples', axis=0, tiled=False)  210 us
    psum x1, blocking collectives, on_device(): lax.psum((jnp.sum(called, axis=0), jnp.sum((genotypes == 1).astype(jnp.fl...  51.5 us
    psum x1, blocking collectives, on_device(): lax.psum((w_sum_part, first_part, second_part, classes), 'samples')  38.9 us
    reduce_sum x1, other arithmetic, on_device(): summed = parts.sum(axis=0)  8.08 us
    ppermute x1, waiting for transfers between devices, shifted(): return lax.ppermute(value, axis, pairs)  7.75 us
  transfers between devices with their start and end apart: 2, of which 2 were waited for; matrix products, arithmetic and copies ran while one was open for 1% of the time, Pallas kernels for 0%

profile of v1, /device:TPU:0, one launch (start us, length us, event | category | flops | bytes accessed | tf_op | source)
XLA Modules:
  0.0 358.5 jit_solution(4264397444789731672)
XLA Ops:
  7.2 0.0 copy-start.1
  7.2 0.0 all-gather.3.cloned.1.call-start
  7.2 0.0 copy-start
  7.2 5.0 %convert_reduce_fusion = (f32[4096]{0:T(1024)S(1)}, f32[512]{0:T(512)S(1)}) fusion(s32[512,4096]{1,0:T(8,128)} %param.2), kind=kLoop, calls=%fused_computation | loop fusion | flops 8384000 | bytes 8407040 | tf_op jit(solution)/shard_map/reduce_sum | solution.py:48
  12.3 0.0 copy-done.1
  12.3 0.7 copy-done
  13.0 6.3 %fusion.2 = (f32[512]{0:T(512)S(1)}, f32[512]{0:T(512)S(1)}, f32[512]{0:T(512)S(1)}, f32[4096]{0:T(1024)S(1)}, f32[512]{0:T(512)S(1)}, /*index=5*/f32[512]{0:T(512)S(1)}, f32[512]{0:T(512)S(1)}) fusion(s32[512,4096]{1,0:T(8,128)S(1)} %copy-done, f32[4096]{0:T(1024)S(1)} %copy-done.1), kind=kLoop, calls=%fused_computation.6 | loop fusion | flops 41935872 | bytes 8433664 | tf_op jit(solution)/shard_map/reduce_sum | solution.py:23
  19.4 38.9 %all-reduce = (f32[512]{0:T(512)S(1)}, f32[512]{0:T(512)S(1)}, f32[512]{0:T(512)S(1)}, f32[4,512]{1,0:T(4,128)S(1)}) all-reduce(f32[512]{0:T(512)S(1)} %get-tuple-element.8, f32[512]{0:T(512)S(1)} %get-tuple-element.7, f32[512]{0:T(512)S(1)} %get-tuple-element.6, ...), channel_id=1, replica_groups=mesh['samples'=8,'variants'=4] {'samples'}, use_global_device_ids=true, to_apply=%region_1.2 | all-reduce | flops 3584 | bytes 28672 | tf_op jit(solution)/shard_map/psum | solution.py:24
  58.2 0.6 multiply_rsqrt_fusion
  58.8 0.0 copy-start.2
  58.8 5.2 %multiply_reduce_fusion = (f32[4096]{0:T(1024)S(1)}, bf16[512,4096]{1,0:T(8,128)(2,1)S(1)}) fusion(f32[512]{0:T(512)S(1)} %get-tuple-element.24, f32[512]{0:T(512)S(1)} %get-tuple-element.26, s32[512,4096]{1,0:T(8,128)} %param.2, f32[4096]{0:T(1024)S(1)} %sqrt.6), kind=kLoop, calls=%fused_computation.11 | loop fusion | flops 23064576 | bytes 12619776 | tf_op jit(solution)/shard_map/reduce_sum | solution.py:49
  64.0 1.3 collective-permute-start
  65.3 7.8 %collective-permute-done = bf16[512,4096]{1,0:T(8,128)(2,1)S(1)} collective-permute-done((bf16[512,4096]{1,0:T(8,128)(2,1)S(1)}, bf16[512,4096]{1,0:T(8,128)(2,1)S(1)}, u32[]{:S(2)}, u32[]{:S(2)}) %collective-permute-start) | collective-permute-done | bytes 4194336 | tf_op jit(solution)/shard_map/ppermute | solution.py:10
  73.1 5.9 %fusion.3 = f32[1024,512]{1,0:T(8,128)} fusion(bf16[512,4096]{1,0:T(8,128)(2,1)S(1)} %get-tuple-element.23, bf16[512,4096]{1,0:T(8,128)(2,1)S(1)} %collective-permute-done), kind=kOutput, calls=%fused_computation.7 | convolution fusion | flops 4311744512 | bytes 10485760 | tf_op jit(solution)/shard_map/dot_general | solution.py:36
  78.9 0.0 copy-done.2
  78.9 0.0 all-gather.3.cloned.1.call-update
  78.9 0.6 convert_element_type.36
  79.6 51.5 %all-reduce.1 = (f32[1,4096]{1,0:T(1,128)S(1)}, f32[1,4096]{1,0:T(1,128)S(1)}, f32[4096]{0:T(1024)S(1)}) all-reduce(f32[1,4096]{1,0:T(1,128)S(1)} %bitcast.9, f32[1,4096]{1,0:T(1,128)S(1)} %bitcast.10, f32[4096]{0:T(1024)S(1)} %get-tuple-element.22), channel_id=1, replica_groups=mesh['samples'=8,'variants'=4] {'variants'}, use_global_device_ids=true, to_apply=%region_15.16 | all-reduce | flops 12288 | bytes 98304 | tf_op jit(solution)/shard_map/psum | solution.py:45
  131.1 0.6 broadcast_multiply_fusion
  131.7 0.7 maximum_convert_fusion
  132.4 210.4 %all-gather.3.cloned.1.call-done = f32[8192,512]{1,0:T(8,128)} async-done(((f32[1024,512]{1,0:T(8,128)}), f32[8192,512]{1,0:T(8,128)}) %all-gather.3.cloned.1.call-update) | async-done | bytes 16777232 | tf_op jit(solution)/shard_map/all_gather | solution.py:39
  342.8 8.1 %reduce_sum.106 = f32[1024,512]{1,0:T(8,128)S(1)} reduce(f32[8,1024,512]{2,1,0:T(8,128)} %bitcast.8, f32[]{:T(128)} %constant.12.clone.1), dimensions={0}, to_apply=%region_11.12 | reduce | flops 3670016 | bytes 18874372 | tf_op jit(solution)/shard_map/reduce_sum | solution.py:40
  350.9 0.7 constant_dynamic-slice_fusion
  (2 shorter events, 0.0 us)
Async XLA Ops:
  7.2 5.1 %copy-start.1 = (f32[4096]{0:T(1024)S(1)}, f32[4096]{0:T(1024)}, u32[]{:S(2)}) copy-start(f32[4096]{0:T(1024)} %param.3) | copy-start | bytes 49156
  7.2 335.6 %all-gather.3.cloned.1.call-start = ((), (), s32[]{:S(2)}) async-start(), calls=%async_computation | async-start | bytes 18874368 | tf_op jit(solution)/shard_map/all_gather | solution.py:39
  7.2 5.8 %copy-start = (s32[512,4096]{1,0:T(8,128)S(1)}, s32[512,4096]{1,0:T(8,128)}, u32[]{:S(2)}) copy-start(s32[512,4096]{1,0:T(8,128)} %param.2) | copy-start | bytes 25165828
  58.8 20.1 %copy-start.2 = (f32[512]{0:T(512)}, f32[512]{0:T(512)S(1)}, u32[]{:S(2)}) copy-start(f32[512]{0:T(512)S(1)} %get-tuple-element.26) | copy-start | bytes 6148
  64.0 9.1 %collective-permute-start = (bf16[512,4096]{1,0:T(8,128)(2,1)S(1)}, bf16[512,4096]{1,0:T(8,128)(2,1)S(1)}, u32[]{:S(2)}, u32[]{:S(2)}) collective-permute-start(bf16[512,4096]{1,0:T(8,128)(2,1)S(1)} %get-tuple-element.23), channel_id=1, source_target_pairs={{1,0},{2,1},{3,2},{5,4},{6,5},{7,6},{9,8},{10,9},{11,10},{13,12},{... | collective-permute-start | bytes 12582920 | tf_op jit(solution)/shard_map/ppermute | solution.py:10
Sparse Core Ops, SparseCore 0:
  79.1 263.6 all-gather.2
